TPU v7x, 512 devices: a whole 4x4x16 slice. The times are simulated.
512 devices in a mesh: gx: 32 (over y, x, core), gy: 16 (over z).
Axes of the slice: x: 4, y: 4, z: 16, core: 2. Of those that a mesh axis runs over, the one named last changes fastest.
Arguments:
- snapshots: bfloat16 [131072, 2048], P(('gx', 'gy')), may hold values from -6 to 6
- volume: bfloat16 [65536, 2048], P('gx', 'gy'), may hold values from -6 to 6
- start_basis: bfloat16 [64, 131072], P(None, ('gx', 'gy')), may hold values from -6 to 6
- wake_mask: int32 [2048], P(('gx', 'gy')), may hold values 0 or 1
Outputs:
- plane_modes: float32 [64, 131072], P(None, ('gx', 'gy'))
- wake_modes: float32 [64, 65536], P(None, ('gx', 'gy'))
All inputs are finite; a program needn't handle non-finite values. No bound on the sum of `wake_mask` on one device may be relied on, other than what follows from the above.
Results may differ from a plain program's by a relative error of at most 0.018.
Values may be sent and summed in bfloat16 or wider, within the bound.
No kernel may reach another device: no remote copies, remote signals or barrier semaphores. Data moves between devices by JAX's collectives and lax.ppermute only.
A program may use at most 64 MiB of HBM per device.

v0:
```python
import jax
import jax.numpy as jnp
from jax import lax
from jax.sharding import Mesh
from jax.sharding import PartitionSpec as P

ITERS = 3
CBLOCK = 32
GX_GY = ("gx_0", "gx_1", "gx_2", "gy")
GX = ("gx_0", "gx_1", "gx_2")


def one_axis_at_a_time(array, axes):
    for axis in axes:
        array = lax.psum(array, axis)
    return array


def cut_along(array, dim, count):
    lengths = array.shape
    tiles = array.reshape(*lengths[:dim], count, lengths[dim] // count, *lengths[dim + 1 :])
    return jnp.moveaxis(tiles, dim, 0)


def sent_and_summed(array, axis, dim):
    tiles = cut_along(array, dim, lax.axis_size(axis))
    arrived = lax.all_to_all(tiles, axis, split_axis=0, concat_axis=0, tiled=True)
    return arrived.sum(axis=0)


def summed_rows(array, axes, dim):
    far, near = axes
    tiles = cut_along(array, dim, lax.axis_size(far))
    nearer = sent_and_summed(tiles, near, dim + 1)
    arrived = lax.all_to_all(nearer, far, split_axis=0, concat_axis=0, tiled=True)
    return arrived.sum(axis=0)


def filled_up(lines, count):
    spare = -len(lines) % count
    return jnp.pad(lines, [(0, spare)] + [(0, 0)] * (lines.ndim - 1))


def copy_for_each(array, axis):
    copies = jnp.broadcast_to(array, (lax.axis_size(axis), *array.shape))
    return lax.all_to_all(copies, axis, split_axis=0, concat_axis=0, tiled=True)


def laid_out(tiles, dim):
    tiles = jnp.moveaxis(tiles, 0, dim)
    lengths = tiles.shape
    return tiles.reshape(*lengths[:dim], lengths[dim] * lengths[dim + 1], *lengths[dim + 2 :])


def gather_axes(array, axes, dim):
    far, near = axes
    tiles = copy_for_each(copy_for_each(array, far), near)
    return laid_out(tiles.swapaxes(0, 1).reshape(-1, *array.shape), dim)


def sum_by_parts(array, axes):
    lines = array.reshape(-1)
    own = summed_rows(filled_up(lines, lax.axis_size(axes[0]) * lax.axis_size(axes[1])), axes, 0)
    whole = gather_axes(own, axes, 0)
    return whole[: len(lines)].reshape(array.shape)


def triangular(lower, right):
    return jax.scipy.linalg.solve_triangular(lower, right, lower=True)


def temporal_weights(basis, snapshots):
    gram_part = jnp.dot(basis, basis.T, preferred_element_type=jnp.float32)
    coeff_part = jnp.dot(basis, snapshots, preferred_element_type=jnp.float32)
    gram = one_axis_at_a_time(gram_part, GX_GY)
    lower = jnp.linalg.cholesky(gram)
    weights = sum_by_parts(triangular(lower, coeff_part), (("gx_0", "gx_1"), ("gx_2", "gy")))
    return (lower, weights)


def local(snapshots, volume, start_basis, wake_mask):
    basis = start_basis
    for step in range(ITERS):
        lower, weights = temporal_weights(basis, snapshots)
        weights_b = weights.astype(jnp.bfloat16)
        basis = lax.dot_general(
            weights_b, snapshots, (((1,), (1,)), ((), ())), preferred_element_type=jnp.float32
        ).astype(jnp.bfloat16)
    lower, weights = temporal_weights(basis, snapshots)
    total_points = snapshots.shape[0] * lax.axis_size(GX) * lax.axis_size("gy")
    plane_modes = triangular(lower, basis.astype(jnp.float32)) * jnp.sqrt(jnp.float32(total_points))
    norms = jnp.sqrt(jnp.sum(weights * weights, axis=1, keepdims=True))
    scaled = (weights / norms).astype(jnp.bfloat16)
    own_cells = lax.all_to_all(volume, "gy", split_axis=0, concat_axis=1, tiled=True)
    projection = lax.dot_general(
        scaled, own_cells, (((1,), (1,)), ((), ())), preferred_element_type=jnp.float32
    )
    cell_mask = jnp.repeat(wake_mask, CBLOCK).astype(jnp.float32)
    return (plane_modes, projection * cell_mask[None, :])


def solution(mesh):
    finer = Mesh(mesh.devices.reshape(4, 4, 2, mesh.shape["gy"]), ("gx_0", "gx_1", "gx_2", "gy"))
    placed = (P(GX_GY, None), P(GX, "gy"), P(None, GX_GY), P(GX_GY))
    return jax.shard_map(
        local,
        mesh=finer,
        in_specs=placed,
        out_specs=(P(None, GX_GY), P(None, GX_GY)),
        check_vma=False,
    )
```

profile of v0, /device:TPU:33, one launch (start us, length us, event | category | flops | bytes accessed | tf_op | source)
XLA Modules:
  0.0 810.4 jit_solution(11774204600463809200)
XLA Ops:
  0.6 1.0 fusion.25
  1.6 13.6 %psum.112 = f32[64,64]{0,1:T(8,128)S(1)} all-reduce(f32[64,64]{0,1:T(8,128)S(1)} %fusion.25), channel_id=1, replica_groups=mesh['gx_0'=4,'gx_1'=4,'gx_2'=2,'gy'=16] {'gx_0'}, use_global_device_ids=true, to_apply=%region_0.0 | all-reduce | flops 4096 | bytes 32768 | tf_op jit(solution)/shard_map/psum | solution.py:15
  15.2 13.3 %psum.113 = f32[64,64]{0,1:T(8,128)S(1)} all-reduce(f32[64,64]{0,1:T(8,128)S(1)} %psum.112), channel_id=1, replica_groups=mesh['gx_0'=4,'gx_1'=4,'gx_2'=2,'gy'=16] {'gx_1'}, use_global_device_ids=true, to_apply=%region_1.0 | all-reduce | flops 4096 | bytes 32768 | tf_op jit(solution)/shard_map/psum | solution.py:15
  28.5 11.4 %psum.114 = f32[64,64]{0,1:T(8,128)S(1)} all-reduce(f32[64,64]{0,1:T(8,128)S(1)} %psum.113), channel_id=1, replica_groups=mesh['gx_0'=4,'gx_1'=4,'gx_2'=2,'gy'=16] {'gx_2'}, use_global_device_ids=true, to_apply=%region_2.0 | all-reduce | flops 4096 | bytes 32768 | tf_op jit(solution)/shard_map/psum | solution.py:15
  40.0 45.1 %psum.115 = f32[64,64]{0,1:T(8,128)S(1)} all-reduce(f32[64,64]{0,1:T(8,128)S(1)} %psum.114), channel_id=1, replica_groups=mesh['gx_0'=4,'gx_1'=4,'gx_2'=2,'gy'=16] {'gy'}, use_global_device_ids=true, to_apply=%region_3.0 | all-reduce | flops 4096 | bytes 32768 | tf_op jit(solution)/shard_map/psum | solution.py:15
  85.1 5.8 cholesky.74
  91.0 0.6 compare_reduce_fusion.3
  91.7 0.7 fusion.2
  92.3 4.9 custom-call.13
  97.6 0.6 fusion.16
  98.6 55.1 %all_to_all.131 = f32[32,16,256]{2,1,0:T(8,128)S(1)} all-to-all(f32[32,16,256]{2,1,0:T(8,128)S(1)} %bitcast.116), channel_id=1, replica_groups=mesh['gx_0'=4,'gx_1'=4,'gx_2'=2,'gy'=16] {'gx_2','gy'}, dimensions={0} | all-to-all | bytes 1048576 | tf_op jit(solution)/shard_map/all_to_all | solution.py:27
  153.7 9.7 %all_to_all.132 = f32[16,1,256]{2,1,0:T(1,128)S(1)} all-to-all(f32[16,1,256]{2,1,0:T(1,128)S(1)} %all_to_all.87), channel_id=1, replica_groups=mesh['gx_0'=4,'gx_1'=4,'gx_2'=2,'gy'=16] {'gx_0','gx_1'}, dimensions={0} | all-to-all | bytes 32768 | tf_op jit(solution)/shard_map/all_to_all | solution.py:35
  163.4 0.5 broadcast.69
  163.9 0.7 reduce.10
  164.6 9.5 %all_to_all.133 = bf16[16,2,128]{2,1,0:T(2,128)(2,1)S(1)} all-to-all(bf16[16,2,128]{2,1,0:T(2,128)(2,1)S(1)} %reshape.72), channel_id=1, replica_groups=mesh['gx_0'=4,'gx_1'=4,'gx_2'=2,'gy'=16] {'gx_0','gx_1'}, dimensions={0} | all-to-all | bytes 16384 | tf_op jit(solution)/shard_map/all_to_all | solution.py:46
  174.2 27.7 %all_to_all.134 = bf16[32,16,256]{2,1,0:T(8,128)(2,1)S(1)} all-to-all(bf16[32,16,256]{2,1,0:T(8,128)(2,1)S(1)} %broadcast_in_dim.31), channel_id=1, replica_groups=mesh['gx_0'=4,'gx_1'=4,'gx_2'=2,'gy'=16] {'gx_2','gy'}, dimensions={0} | all-to-all | bytes 524288 | tf_op jit(solution)/shard_map/all_to_all | solution.py:46
  202.1 0.4 convolution_convert_fusion.2
  203.0 11.7 %psum.116 = f32[64,64]{0,1:T(8,128)S(1)} all-reduce(f32[64,64]{0,1:T(8,128)S(1)} %fusion.27), channel_id=1, replica_groups=mesh['gx_0'=4,'gx_1'=4,'gx_2'=2,'gy'=16] {'gx_0'}, use_global_device_ids=true, to_apply=%region_8.11 | all-reduce | flops 4096 | bytes 32768 | tf_op jit(solution)/shard_map/psum | solution.py:15
  214.7 11.7 %psum.117 = f32[64,64]{0,1:T(8,128)S(1)} all-reduce(f32[64,64]{0,1:T(8,128)S(1)} %psum.116), channel_id=1, replica_groups=mesh['gx_0'=4,'gx_1'=4,'gx_2'=2,'gy'=16] {'gx_1'}, use_global_device_ids=true, to_apply=%region_9.12 | all-reduce | flops 4096 | bytes 32768 | tf_op jit(solution)/shard_map/psum | solution.py:15
  226.5 10.5 %psum.118 = f32[64,64]{0,1:T(8,128)S(1)} all-reduce(f32[64,64]{0,1:T(8,128)S(1)} %psum.117), channel_id=1, replica_groups=mesh['gx_0'=4,'gx_1'=4,'gx_2'=2,'gy'=16] {'gx_2'}, use_global_device_ids=true, to_apply=%region_10.13 | all-reduce | flops 4096 | bytes 32768 | tf_op jit(solution)/shard_map/psum | solution.py:15
  237.0 38.3 %psum.119 = f32[64,64]{0,1:T(8,128)S(1)} all-reduce(f32[64,64]{0,1:T(8,128)S(1)} %psum.118), channel_id=1, replica_groups=mesh['gx_0'=4,'gx_1'=4,'gx_2'=2,'gy'=16] {'gy'}, use_global_device_ids=true, to_apply=%region_11.14 | all-reduce | flops 4096 | bytes 32768 | tf_op jit(solution)/shard_map/psum | solution.py:15
  275.4 5.8 cholesky.85
  281.3 0.6 compare_reduce_fusion.2
  281.9 0.7 fusion.3
  282.6 4.9 custom-call.14
  287.5 0.6 fusion.13
  288.5 53.1 %all_to_all.135 = f32[32,16,256]{2,1,0:T(8,128)S(1)} all-to-all(f32[32,16,256]{2,1,0:T(8,128)S(1)} %bitcast.117), channel_id=1, replica_groups=mesh['gx_0'=4,'gx_1'=4,'gx_2'=2,'gy'=16] {'gx_2','gy'}, dimensions={0} | all-to-all | bytes 1048576 | tf_op jit(solution)/shard_map/all_to_all | solution.py:27
  341.7 9.7 %all_to_all.136 = f32[16,1,256]{2,1,0:T(1,128)S(1)} all-to-all(f32[16,1,256]{2,1,0:T(1,128)S(1)} %all_to_all.93), channel_id=1, replica_groups=mesh['gx_0'=4,'gx_1'=4,'gx_2'=2,'gy'=16] {'gx_0','gx_1'}, dimensions={0} | all-to-all | bytes 32768 | tf_op jit(solution)/shard_map/all_to_all | solution.py:35
  351.4 0.7 reduce.11
  352.1 9.5 %all_to_all.137 = bf16[16,2,128]{2,1,0:T(2,128)(2,1)S(1)} all-to-all(bf16[16,2,128]{2,1,0:T(2,128)(2,1)S(1)} %reshape.74), channel_id=1, replica_groups=mesh['gx_0'=4,'gx_1'=4,'gx_2'=2,'gy'=16] {'gx_0','gx_1'}, dimensions={0} | all-to-all | bytes 16384 | tf_op jit(solution)/shard_map/all_to_all | solution.py:46
  361.6 27.8 %all_to_all.138 = bf16[32,16,256]{2,1,0:T(8,128)(2,1)S(1)} all-to-all(bf16[32,16,256]{2,1,0:T(8,128)(2,1)S(1)} %broadcast_in_dim.33), channel_id=1, replica_groups=mesh['gx_0'=4,'gx_1'=4,'gx_2'=2,'gy'=16] {'gx_2','gy'}, dimensions={0} | all-to-all | bytes 524288 | tf_op jit(solution)/shard_map/all_to_all | solution.py:46
  390.5 11.7 %psum.120 = f32[64,64]{0,1:T(8,128)S(1)} all-reduce(f32[64,64]{0,1:T(8,128)S(1)} %fusion.29), channel_id=1, replica_groups=mesh['gx_0'=4,'gx_1'=4,'gx_2'=2,'gy'=16] {'gx_0'}, use_global_device_ids=true, to_apply=%region_14.17 | all-reduce | flops 4096 | bytes 32768 | tf_op jit(solution)/shard_map/psum | solution.py:15
  402.2 11.7 %psum.121 = f32[64,64]{0,1:T(8,128)S(1)} all-reduce(f32[64,64]{0,1:T(8,128)S(1)} %psum.120), channel_id=1, replica_groups=mesh['gx_0'=4,'gx_1'=4,'gx_2'=2,'gy'=16] {'gx_1'}, use_global_device_ids=true, to_apply=%region_15.18 | all-reduce | flops 4096 | bytes 32768 | tf_op jit(solution)/shard_map/psum | solution.py:15
  413.9 10.5 %psum.122 = f32[64,64]{0,1:T(8,128)S(1)} all-reduce(f32[64,64]{0,1:T(8,128)S(1)} %psum.121), channel_id=1, replica_groups=mesh['gx_0'=4,'gx_1'=4,'gx_2'=2,'gy'=16] {'gx_2'}, use_global_device_ids=true, to_apply=%region_16.19 | all-reduce | flops 4096 | bytes 32768 | tf_op jit(solution)/shard_map/psum | solution.py:15
  424.4 38.9 %psum.123 = f32[64,64]{0,1:T(8,128)S(1)} all-reduce(f32[64,64]{0,1:T(8,128)S(1)} %psum.122), channel_id=1, replica_groups=mesh['gx_0'=4,'gx_1'=4,'gx_2'=2,'gy'=16] {'gy'}, use_global_device_ids=true, to_apply=%region_17.20 | all-reduce | flops 4096 | bytes 32768 | tf_op jit(solution)/shard_map/psum | solution.py:15
  463.4 5.8 cholesky.96
  469.3 0.6 compare_reduce_fusion.1
  469.9 0.7 fusion.4
  470.6 4.9 custom-call.15
  475.5 0.6 fusion.10
  476.5 52.5 %all_to_all.139 = f32[32,16,256]{2,1,0:T(8,128)S(1)} all-to-all(f32[32,16,256]{2,1,0:T(8,128)S(1)} %bitcast.118), channel_id=1, replica_groups=mesh['gx_0'=4,'gx_1'=4,'gx_2'=2,'gy'=16] {'gx_2','gy'}, dimensions={0} | all-to-all | bytes 1048576 | tf_op jit(solution)/shard_map/all_to_all | solution.py:27
  529.1 9.7 %all_to_all.140 = f32[16,1,256]{2,1,0:T(1,128)S(1)} all-to-all(f32[16,1,256]{2,1,0:T(1,128)S(1)} %all_to_all.99), channel_id=1, replica_groups=mesh['gx_0'=4,'gx_1'=4,'gx_2'=2,'gy'=16] {'gx_0','gx_1'}, dimensions={0} | all-to-all | bytes 32768 | tf_op jit(solution)/shard_map/all_to_all | solution.py:35
  538.8 0.7 reduce.12
  539.5 9.5 %all_to_all.141 = bf16[16,2,128]{2,1,0:T(2,128)(2,1)S(1)} all-to-all(bf16[16,2,128]{2,1,0:T(2,128)(2,1)S(1)} %reshape.76), channel_id=1, replica_groups=mesh['gx_0'=4,'gx_1'=4,'gx_2'=2,'gy'=16] {'gx_0','gx_1'}, dimensions={0} | all-to-all | bytes 16384 | tf_op jit(solution)/shard_map/all_to_all | solution.py:46
  549.0 27.7 %all_to_all.142 = bf16[32,16,256]{2,1,0:T(8,128)(2,1)S(1)} all-to-all(bf16[32,16,256]{2,1,0:T(8,128)(2,1)S(1)} %broadcast_in_dim.35), channel_id=1, replica_groups=mesh['gx_0'=4,'gx_1'=4,'gx_2'=2,'gy'=16] {'gx_2','gy'}, dimensions={0} | all-to-all | bytes 524288 | tf_op jit(solution)/shard_map/all_to_all | solution.py:46
  577.9 11.7 %psum.124 = f32[64,64]{0,1:T(8,128)S(1)} all-reduce(f32[64,64]{0,1:T(8,128)S(1)} %fusion.31), channel_id=1, replica_groups=mesh['gx_0'=4,'gx_1'=4,'gx_2'=2,'gy'=16] {'gx_0'}, use_global_device_ids=true, to_apply=%region_20.23 | all-reduce | flops 4096 | bytes 32768 | tf_op jit(solution)/shard_map/psum | solution.py:15
  589.6 11.7 %psum.125 = f32[64,64]{0,1:T(8,128)S(1)} all-reduce(f32[64,64]{0,1:T(8,128)S(1)} %psum.124), channel_id=1, replica_groups=mesh['gx_0'=4,'gx_1'=4,'gx_2'=2,'gy'=16] {'gx_1'}, use_global_device_ids=true, to_apply=%region_21.24 | all-reduce | flops 4096 | bytes 32768 | tf_op jit(solution)/shard_map/psum | solution.py:15
  601.3 10.5 %psum.126 = f32[64,64]{0,1:T(8,128)S(1)} all-reduce(f32[64,64]{0,1:T(8,128)S(1)} %psum.125), channel_id=1, replica_groups=mesh['gx_0'=4,'gx_1'=4,'gx_2'=2,'gy'=16] {'gx_2'}, use_global_device_ids=true, to_apply=%region_22.25 | all-reduce | flops 4096 | bytes 32768 | tf_op jit(solution)/shard_map/psum | solution.py:15
  611.9 38.3 %psum.127 = f32[64,64]{0,1:T(8,128)S(1)} all-reduce(f32[64,64]{0,1:T(8,128)S(1)} %psum.126), channel_id=1, replica_groups=mesh['gx_0'=4,'gx_1'=4,'gx_2'=2,'gy'=16] {'gy'}, use_global_device_ids=true, to_apply=%region_23.26 | all-reduce | flops 4096 | bytes 32768 | tf_op jit(solution)/shard_map/psum | solution.py:15
  650.2 5.8 cholesky.107
  656.1 0.6 compare_reduce_fusion
  656.8 0.7 fusion.5
  657.4 4.9 custom-call.9
  662.3 0.6 fusion.6
  663.4 53.1 %all_to_all.143 = f32[32,16,256]{2,1,0:T(8,128)S(1)} all-to-all(f32[32,16,256]{2,1,0:T(8,128)S(1)} %bitcast.119), channel_id=1, replica_groups=mesh['gx_0'=4,'gx_1'=4,'gx_2'=2,'gy'=16] {'gx_2','gy'}, dimensions={0} | all-to-all | bytes 1048576 | tf_op jit(solution)/shard_map/all_to_all | solution.py:27
  716.5 9.7 %all_to_all.144 = f32[16,1,256]{2,1,0:T(1,128)S(1)} all-to-all(f32[16,1,256]{2,1,0:T(1,128)S(1)} %all_to_all.105), channel_id=1, replica_groups=mesh['gx_0'=4,'gx_1'=4,'gx_2'=2,'gy'=16] {'gx_0','gx_1'}, dimensions={0} | all-to-all | bytes 32768 | tf_op jit(solution)/shard_map/all_to_all | solution.py:35
  726.2 9.5 %all_to_all.145 = f32[16,1,256]{2,1,0:T(1,128)S(1)} all-to-all(f32[16,1,256]{2,1,0:T(1,128)S(1)} %broadcast_in_dim.36), channel_id=1, replica_groups=mesh['gx_0'=4,'gx_1'=4,'gx_2'=2,'gy'=16] {'gx_0','gx_1'}, dimensions={0} | all-to-all | bytes 32768 | tf_op jit(solution)/shard_map/all_to_all | solution.py:46
  735.7 3.9 all-to-all-start.16
  739.6 23.8 %all-to-all-done.16 = bf16[16,128,128]{2,1,0:T(8,128)(2,1)S(1)} async-done(((bf16[16,128,128]{2,1,0:T(8,128)(2,1)}), bf16[16,128,128]{2,1,0:T(8,128)(2,1)S(1)}, u32[]{:S(2)}, u32[]{:S(2)}) %all-to-all-start.16) | async-done | bytes 524320 | tf_op jit(solution)/shard_map/all_to_all | solution.py:94
  763.3 0.8 broadcast_in_dim.37
  764.2 12.7 %all-to-all-start.15 = ((f32[32,16,256]{2,1,0:T(8,128)}), f32[32,16,256]{2,1,0:T(8,128)S(1)}, u32[]{:S(2)}, u32[]{:S(2)}) async-start(f32[32,16,256]{2,1,0:T(8,128)} %broadcast_in_dim.37), calls=%async_computation.15 | async-start | bytes 1048576 | tf_op jit(solution)/shard_map/all_to_all | solution.py:46
  777.4 0.9 convolution_multiply_fusion
  778.2 30.3 %all-to-all-done.15 = f32[32,16,256]{2,1,0:T(8,128)S(1)} async-done(((f32[32,16,256]{2,1,0:T(8,128)}), f32[32,16,256]{2,1,0:T(8,128)S(1)}, u32[]{:S(2)}, u32[]{:S(2)}) %all-to-all-start.15) | async-done | bytes 524320 | tf_op jit(solution)/shard_map/all_to_all | solution.py:46
  809.5 0.8 convolution_multiply_fusion.1
  (85 shorter events, 7.1 us)
Async XLA Ops:
  0.6 96.6 %copy-start = (bf16[256,2048]{1,0:T(8,128)(2,1)S(1)}, bf16[256,2048]{1,0:T(8,128)(2,1)}, u32[]{:S(2)}) copy-start(bf16[256,2048]{1,0:T(8,128)(2,1)} %param.7) | copy-start | bytes 3145732
  91.7 5.6 copy-start.1
  735.7 27.6 %all-to-all-start.16 = ((bf16[16,128,128]{2,1,0:T(8,128)(2,1)}), bf16[16,128,128]{2,1,0:T(8,128)(2,1)S(1)}, u32[]{:S(2)}, u32[]{:S(2)}) async-start(bf16[16,128,128]{2,1,0:T(8,128)(2,1)} %bitcast.23), calls=%async_computation.16 | async-start | bytes 1048576 | tf_op jit(solution)/shard_map/all_to_all | solution.py:94
  764.2 12.7 %copy-start.2 = (s32[4]{0:T(128)S(1)}, s32[4]{0:T(128)}, u32[]{:S(2)}) copy-start(s32[4]{0:T(128)} %param.10) | copy-start | bytes 52
  764.2 44.3 %all-to-all-start.15 = ((f32[32,16,256]{2,1,0:T(8,128)}), f32[32,16,256]{2,1,0:T(8,128)S(1)}, u32[]{:S(2)}, u32[]{:S(2)}) async-start(f32[32,16,256]{2,1,0:T(8,128)} %broadcast_in_dim.37), calls=%async_computation.15 | async-start | bytes 1048576 | tf_op jit(solution)/shard_map/all_to_all | solution.py:46
where the time goes:
time: 812 us; the launch traced here: 810 us
  blocking collectives  674 us (83%)
  waiting for transfers between devices  54.1 us (7%)
  other arithmetic  51.2 us (6%)
  starting transfers between devices  16.6 us (2%)
  matrix products  8.18 us (1%)
    psum x16, blocking collectives, one_axis_at_a_time(): array = lax.psum(array, axis)  301 us
    all_to_all x4, blocking collectives, sent_and_summed(): lax.all_to_all(tiles, axis, split_axis=0, concat_axis=0, tiled=True)  214 us
    all_to_all x7, blocking collectives, copy_for_each(): return lax.all_to_all(copies, axis, split_axis=0, concat_axis=0, tiled=True)  121 us
    all_to_all x4, blocking collectives, summed_rows(): lax.all_to_all(nearer, far, split_axis=0, concat_axis=0, tiled=True)  38.6 us
    all_to_all x1, waiting for transfers between devices, copy_for_each(): return lax.all_to_all(copies, axis, split_axis=0, concat_axis=0, tiled=True)  30.3 us
    another operation x12, other arithmetic, temporal_weights(): lower = jnp.linalg.cholesky(gram)  26.1 us
    all_to_all x1, waiting for transfers between devices, local(): lax.all_to_all(volume, 'gy', split_axis=0, concat_axis=1, tiled=True)  23.8 us
    another operation x8, other arithmetic, triangular(): return jax.scipy.linalg.solve_triangular(lower, right, lower=True)  22.2 us
  transfers between devices with their start and end apart: 2, of which 2 were waited for; matrix products, arithmetic and copies ran while one was open for 0% of the time, Pallas kernels for 0%

commit v1 on v0

--- a/solution.py
+++ b/solution.py
@@ -12,7 +12,7 @@
 
 def one_axis_at_a_time(array, axes):
     for axis in axes:
-        array = lax.psum(array, axis)
+        array = jnp.sum(lax.all_gather(array, axis), axis=0)
     return array
 
 

time: 812 us -> 682 us (0.84)
  blocking collectives: 674 us -> 545 us
    psum x16 -> x0, blocking collectives: 301 us -> none  [one_axis_at_a_time(): array = lax.psum(array, axis)]
    all_gather x0 -> x16, blocking collectives: none -> 201 us  [one_axis_at_a_time(): array = jnp.sum(lax.all_gather(array, axis), axis=0)]
    all_to_all x4, blocking collectives: 214 us -> 182 us  [sent_and_summed(): lax.all_to_all(tiles, axis, split_axis=0, concat_axis=0, tiled=True)]
where the time goes in v1:
time: 682 us; the launch traced here: 681 us
  blocking collectives  545 us (80%)
  waiting for transfers between devices  54.1 us (8%)
  other arithmetic  51.5 us (8%)
  starting transfers between devices  16.6 us (2%)
  matrix products  8.19 us (1%)
    all_gather x16, blocking collectives, one_axis_at_a_time(): array = jnp.sum(lax.all_gather(array, axis), axis=0)  201 us
    all_to_all x4, blocking collectives, sent_and_summed(): lax.all_to_all(tiles, axis, split_axis=0, concat_axis=0, tiled=True)  182 us
    all_to_all x7, blocking collectives, copy_for_each(): return lax.all_to_all(copies, axis, split_axis=0, concat_axis=0, tiled=True)  121 us
    all_to_all x4, blocking collectives, summed_rows(): lax.all_to_all(nearer, far, split_axis=0, concat_axis=0, tiled=True)  40.8 us
    all_to_all x1, waiting for transfers between devices, copy_for_each(): return lax.all_to_all(copies, axis, split_axis=0, concat_axis=0, tiled=True)  30.3 us
    another operation x12, other arithmetic, temporal_weights(): lower = jnp.linalg.cholesky(gram)  26.1 us
    all_to_all x1, waiting for transfers between devices, local(): lax.all_to_all(volume, 'gy', split_axis=0, concat_axis=1, tiled=True)  23.8 us
    another operation x8, other arithmetic, triangular(): return jax.scipy.linalg.solve_triangular(lower, right, lower=True)  22.2 us
  transfers between devices with their start and end apart: 2, of which 2 were waited for; matrix products, arithmetic and copies ran while one was open for 0% of the time, Pallas kernels for 0%

profile of v1, /device:TPU:33, one launch (start us, length us, event | category | flops | bytes accessed | tf_op | source)
XLA Modules:
  0.0 681.1 jit_solution(10981907031086914121)
XLA Ops:
  0.6 1.0 fusion.25
  1.6 9.7 %all-gather = f32[256,64]{1,0:T(8,128)S(1)} all-gather(f32[64,64]{1,0:T(8,128)S(1)} %fusion.25), channel_id=2, replica_groups=mesh['gx_0'=4,'gx_1'=4,'gx_2'=2,'gy'=16] {'gx_0'}, dimensions={0}, use_global_device_ids=true | all-gather | bytes 81920 | tf_op jit(solution)/shard_map/all_gather | solution.py:15
  11.4 9.5 %all-gather.1 = f32[256,64]{1,0:T(8,128)S(1)} all-gather(f32[64,64]{1,0:T(8,128)S(1)} %reduce_sum.232), channel_id=3, replica_groups=mesh['gx_0'=4,'gx_1'=4,'gx_2'=2,'gy'=16] {'gx_1'}, dimensions={0}, use_global_device_ids=true | all-gather | bytes 81920 | tf_op jit(solution)/shard_map/all_gather | solution.py:15
  20.9 7.8 %all-gather.2 = f32[128,64]{1,0:T(8,128)S(1)} all-gather(f32[64,64]{1,0:T(8,128)S(1)} %reduce_sum.233), channel_id=4, replica_groups=mesh['gx_0'=4,'gx_1'=4,'gx_2'=2,'gy'=16] {'gx_2'}, dimensions={0}, use_global_device_ids=true | all-gather | bytes 49152 | tf_op jit(solution)/shard_map/all_gather | solution.py:15
  28.7 29.4 %all-gather.3 = f32[1024,64]{1,0:T(8,128)S(1)} all-gather(f32[64,64]{1,0:T(8,128)S(1)} %reduce_sum.234), channel_id=5, replica_groups=mesh['gx_0'=4,'gx_1'=4,'gx_2'=2,'gy'=16] {'gy'}, dimensions={0}, use_global_device_ids=true | all-gather | bytes 278528 | tf_op jit(solution)/shard_map/all_gather | solution.py:15
  58.3 5.8 cholesky.74
  64.2 0.6 compare_reduce_fusion.3
  64.8 0.7 fusion.2
  65.5 4.9 custom-call.13
  70.7 0.6 fusion.16
  71.8 47.5 %all_to_all.131 = f32[32,16,256]{2,1,0:T(8,128)S(1)} all-to-all(f32[32,16,256]{2,1,0:T(8,128)S(1)} %bitcast.136), channel_id=1, replica_groups=mesh['gx_0'=4,'gx_1'=4,'gx_2'=2,'gy'=16] {'gx_2','gy'}, dimensions={0} | all-to-all | bytes 1048576 | tf_op jit(solution)/shard_map/all_to_all | solution.py:27
  119.3 11.7 %all_to_all.132 = f32[16,1,256]{2,1,0:T(1,128)S(1)} all-to-all(f32[16,1,256]{2,1,0:T(1,128)S(1)} %all_to_all.87), channel_id=1, replica_groups=mesh['gx_0'=4,'gx_1'=4,'gx_2'=2,'gy'=16] {'gx_0','gx_1'}, dimensions={0} | all-to-all | bytes 32768 | tf_op jit(solution)/shard_map/all_to_all | solution.py:35
  131.0 0.5 broadcast.69
  131.5 0.7 reduce.10
  132.3 9.5 %all_to_all.133 = bf16[16,2,128]{2,1,0:T(2,128)(2,1)S(1)} all-to-all(bf16[16,2,128]{2,1,0:T(2,128)(2,1)S(1)} %reshape.88), channel_id=1, replica_groups=mesh['gx_0'=4,'gx_1'=4,'gx_2'=2,'gy'=16] {'gx_0','gx_1'}, dimensions={0} | all-to-all | bytes 16384 | tf_op jit(solution)/shard_map/all_to_all | solution.py:46
  141.8 27.7 %all_to_all.134 = bf16[32,16,256]{2,1,0:T(8,128)(2,1)S(1)} all-to-all(bf16[32,16,256]{2,1,0:T(8,128)(2,1)S(1)} %broadcast_in_dim.31), channel_id=1, replica_groups=mesh['gx_0'=4,'gx_1'=4,'gx_2'=2,'gy'=16] {'gx_2','gy'}, dimensions={0} | all-to-all | bytes 524288 | tf_op jit(solution)/shard_map/all_to_all | solution.py:46
  170.6 9.1 %all-gather.4 = f32[256,64]{1,0:T(8,128)S(1)} all-gather(f32[64,64]{1,0:T(8,128)S(1)} %fusion.27), channel_id=6, replica_groups=mesh['gx_0'=4,'gx_1'=4,'gx_2'=2,'gy'=16] {'gx_0'}, dimensions={0}, use_global_device_ids=true | all-gather | bytes 81920 | tf_op jit(solution)/shard_map/all_gather | solution.py:15
  179.7 9.1 %all-gather.5 = f32[256,64]{1,0:T(8,128)S(1)} all-gather(f32[64,64]{1,0:T(8,128)S(1)} %reduce_sum.238), channel_id=7, replica_groups=mesh['gx_0'=4,'gx_1'=4,'gx_2'=2,'gy'=16] {'gx_1'}, dimensions={0}, use_global_device_ids=true | all-gather | bytes 81920 | tf_op jit(solution)/shard_map/all_gather | solution.py:15
  188.9 7.1 %all-gather.6 = f32[128,64]{1,0:T(8,128)S(1)} all-gather(f32[64,64]{1,0:T(8,128)S(1)} %reduce_sum.239), channel_id=8, replica_groups=mesh['gx_0'=4,'gx_1'=4,'gx_2'=2,'gy'=16] {'gx_2'}, dimensions={0}, use_global_device_ids=true | all-gather | bytes 49152 | tf_op jit(solution)/shard_map/all_gather | solution.py:15
  195.9 22.8 %all-gather.7 = f32[1024,64]{1,0:T(8,128)S(1)} all-gather(f32[64,64]{1,0:T(8,128)S(1)} %reduce_sum.240), channel_id=9, replica_groups=mesh['gx_0'=4,'gx_1'=4,'gx_2'=2,'gy'=16] {'gy'}, dimensions={0}, use_global_device_ids=true | all-gather | bytes 278528 | tf_op jit(solution)/shard_map/all_gather | solution.py:15
  218.9 5.8 cholesky.85
  224.8 0.6 compare_reduce_fusion.2
  225.4 0.7 fusion.3
  226.1 4.9 custom-call.14
  231.0 0.6 fusion.13
  232.0 44.8 %all_to_all.135 = f32[32,16,256]{2,1,0:T(8,128)S(1)} all-to-all(f32[32,16,256]{2,1,0:T(8,128)S(1)} %bitcast.137), channel_id=1, replica_groups=mesh['gx_0'=4,'gx_1'=4,'gx_2'=2,'gy'=16] {'gx_2','gy'}, dimensions={0} | all-to-all | bytes 1048576 | tf_op jit(solution)/shard_map/all_to_all | solution.py:27
  276.9 9.7 %all_to_all.136 = f32[16,1,256]{2,1,0:T(1,128)S(1)} all-to-all(f32[16,1,256]{2,1,0:T(1,128)S(1)} %all_to_all.93), channel_id=1, replica_groups=mesh['gx_0'=4,'gx_1'=4,'gx_2'=2,'gy'=16] {'gx_0','gx_1'}, dimensions={0} | all-to-all | bytes 32768 | tf_op jit(solution)/shard_map/all_to_all | solution.py:35
  286.6 0.7 reduce.11
  287.4 9.5 %all_to_all.137 = bf16[16,2,128]{2,1,0:T(2,128)(2,1)S(1)} all-to-all(bf16[16,2,128]{2,1,0:T(2,128)(2,1)S(1)} %reshape.90), channel_id=1, replica_groups=mesh['gx_0'=4,'gx_1'=4,'gx_2'=2,'gy'=16] {'gx_0','gx_1'}, dimensions={0} | all-to-all | bytes 16384 | tf_op jit(solution)/shard_map/all_to_all | solution.py:46
  296.9 27.7 %all_to_all.138 = bf16[32,16,256]{2,1,0:T(8,128)(2,1)S(1)} all-to-all(bf16[32,16,256]{2,1,0:T(8,128)(2,1)S(1)} %broadcast_in_dim.33), channel_id=1, replica_groups=mesh['gx_0'=4,'gx_1'=4,'gx_2'=2,'gy'=16] {'gx_2','gy'}, dimensions={0} | all-to-all | bytes 524288 | tf_op jit(solution)/shard_map/all_to_all | solution.py:46
  325.7 9.1 %all-gather.8 = f32[256,64]{1,0:T(8,128)S(1)} all-gather(f32[64,64]{1,0:T(8,128)S(1)} %fusion.29), channel_id=10, replica_groups=mesh['gx_0'=4,'gx_1'=4,'gx_2'=2,'gy'=16] {'gx_0'}, dimensions={0}, use_global_device_ids=true | all-gather | bytes 81920 | tf_op jit(solution)/shard_map/all_gather | solution.py:15
  334.8 9.1 %all-gather.9 = f32[256,64]{1,0:T(8,128)S(1)} all-gather(f32[64,64]{1,0:T(8,128)S(1)} %reduce_sum.244), channel_id=11, replica_groups=mesh['gx_0'=4,'gx_1'=4,'gx_2'=2,'gy'=16] {'gx_1'}, dimensions={0}, use_global_device_ids=true | all-gather | bytes 81920 | tf_op jit(solution)/shard_map/all_gather | solution.py:15
  344.0 7.1 %all-gather.10 = f32[128,64]{1,0:T(8,128)S(1)} all-gather(f32[64,64]{1,0:T(8,128)S(1)} %reduce_sum.245), channel_id=12, replica_groups=mesh['gx_0'=4,'gx_1'=4,'gx_2'=2,'gy'=16] {'gx_2'}, dimensions={0}, use_global_device_ids=true | all-gather | bytes 49152 | tf_op jit(solution)/shard_map/all_gather | solution.py:15
  351.0 23.0 %all-gather.11 = f32[1024,64]{1,0:T(8,128)S(1)} all-gather(f32[64,64]{1,0:T(8,128)S(1)} %reduce_sum.246), channel_id=13, replica_groups=mesh['gx_0'=4,'gx_1'=4,'gx_2'=2,'gy'=16] {'gy'}, dimensions={0}, use_global_device_ids=true | all-gather | bytes 278528 | tf_op jit(solution)/shard_map/all_gather | solution.py:15
  374.2 5.8 cholesky.96
  380.0 0.6 compare_reduce_fusion.1
  380.7 0.7 fusion.4
  381.3 4.9 custom-call.15
  386.2 0.6 fusion.10
  387.3 44.8 %all_to_all.139 = f32[32,16,256]{2,1,0:T(8,128)S(1)} all-to-all(f32[32,16,256]{2,1,0:T(8,128)S(1)} %bitcast.138), channel_id=1, replica_groups=mesh['gx_0'=4,'gx_1'=4,'gx_2'=2,'gy'=16] {'gx_2','gy'}, dimensions={0} | all-to-all | bytes 1048576 | tf_op jit(solution)/shard_map/all_to_all | solution.py:27
  432.2 9.7 %all_to_all.140 = f32[16,1,256]{2,1,0:T(1,128)S(1)} all-to-all(f32[16,1,256]{2,1,0:T(1,128)S(1)} %all_to_all.99), channel_id=1, replica_groups=mesh['gx_0'=4,'gx_1'=4,'gx_2'=2,'gy'=16] {'gx_0','gx_1'}, dimensions={0} | all-to-all | bytes 32768 | tf_op jit(solution)/shard_map/all_to_all | solution.py:35
  441.9 0.7 reduce.12
  442.6 9.5 %all_to_all.141 = bf16[16,2,128]{2,1,0:T(2,128)(2,1)S(1)} all-to-all(bf16[16,2,128]{2,1,0:T(2,128)(2,1)S(1)} %reshape.92), channel_id=1, replica_groups=mesh['gx_0'=4,'gx_1'=4,'gx_2'=2,'gy'=16] {'gx_0','gx_1'}, dimensions={0} | all-to-all | bytes 16384 | tf_op jit(solution)/shard_map/all_to_all | solution.py:46
  452.1 27.7 %all_to_all.142 = bf16[32,16,256]{2,1,0:T(8,128)(2,1)S(1)} all-to-all(bf16[32,16,256]{2,1,0:T(8,128)(2,1)S(1)} %broadcast_in_dim.35), channel_id=1, replica_groups=mesh['gx_0'=4,'gx_1'=4,'gx_2'=2,'gy'=16] {'gx_2','gy'}, dimensions={0} | all-to-all | bytes 524288 | tf_op jit(solution)/shard_map/all_to_all | solution.py:46
  480.1 0.4 convolution_convert_fusion
  481.0 9.1 %all-gather.12 = f32[256,64]{1,0:T(8,128)S(1)} all-gather(f32[64,64]{1,0:T(8,128)S(1)} %fusion.31), channel_id=14, replica_groups=mesh['gx_0'=4,'gx_1'=4,'gx_2'=2,'gy'=16] {'gx_0'}, dimensions={0}, use_global_device_ids=true | all-gather | bytes 81920 | tf_op jit(solution)/shard_map/all_gather | solution.py:15
  490.1 9.1 %all-gather.13 = f32[256,64]{1,0:T(8,128)S(1)} all-gather(f32[64,64]{1,0:T(8,128)S(1)} %reduce_sum.250), channel_id=15, replica_groups=mesh['gx_0'=4,'gx_1'=4,'gx_2'=2,'gy'=16] {'gx_1'}, dimensions={0}, use_global_device_ids=true | all-gather | bytes 81920 | tf_op jit(solution)/shard_map/all_gather | solution.py:15
  499.2 7.1 %all-gather.14 = f32[128,64]{1,0:T(8,128)S(1)} all-gather(f32[64,64]{1,0:T(8,128)S(1)} %reduce_sum.251), channel_id=16, replica_groups=mesh['gx_0'=4,'gx_1'=4,'gx_2'=2,'gy'=16] {'gx_2'}, dimensions={0}, use_global_device_ids=true | all-gather | bytes 49152 | tf_op jit(solution)/shard_map/all_gather | solution.py:15
  506.3 22.8 %all-gather.15 = f32[1024,64]{1,0:T(8,128)S(1)} all-gather(f32[64,64]{1,0:T(8,128)S(1)} %reduce_sum.252), channel_id=17, replica_groups=mesh['gx_0'=4,'gx_1'=4,'gx_2'=2,'gy'=16] {'gy'}, dimensions={0}, use_global_device_ids=true | all-gather | bytes 278528 | tf_op jit(solution)/shard_map/all_gather | solution.py:15
  529.3 5.8 cholesky.107
  535.1 0.6 compare_reduce_fusion
  535.8 0.7 fusion.5
  536.4 4.9 custom-call.9
  541.3 0.6 fusion.6
  542.4 44.8 %all_to_all.143 = f32[32,16,256]{2,1,0:T(8,128)S(1)} all-to-all(f32[32,16,256]{2,1,0:T(8,128)S(1)} %bitcast.139), channel_id=1, replica_groups=mesh['gx_0'=4,'gx_1'=4,'gx_2'=2,'gy'=16] {'gx_2','gy'}, dimensions={0} | all-to-all | bytes 1048576 | tf_op jit(solution)/shard_map/all_to_all | solution.py:27
  587.3 9.7 %all_to_all.144 = f32[16,1,256]{2,1,0:T(1,128)S(1)} all-to-all(f32[16,1,256]{2,1,0:T(1,128)S(1)} %all_to_all.105), channel_id=1, replica_groups=mesh['gx_0'=4,'gx_1'=4,'gx_2'=2,'gy'=16] {'gx_0','gx_1'}, dimensions={0} | all-to-all | bytes 32768 | tf_op jit(solution)/shard_map/all_to_all | solution.py:35
  597.0 9.5 %all_to_all.145 = f32[16,1,256]{2,1,0:T(1,128)S(1)} all-to-all(f32[16,1,256]{2,1,0:T(1,128)S(1)} %broadcast_in_dim.36), channel_id=1, replica_groups=mesh['gx_0'=4,'gx_1'=4,'gx_2'=2,'gy'=16] {'gx_0','gx_1'}, dimensions={0} | all-to-all | bytes 32768 | tf_op jit(solution)/shard_map/all_to_all | solution.py:46
  606.5 3.9 all-to-all-start.16
  610.3 23.8 %all-to-all-done.16 = bf16[16,128,128]{2,1,0:T(8,128)(2,1)S(1)} async-done(((bf16[16,128,128]{2,1,0:T(8,128)(2,1)}), bf16[16,128,128]{2,1,0:T(8,128)(2,1)S(1)}, u32[]{:S(2)}, u32[]{:S(2)}) %all-to-all-start.16) | async-done | bytes 524320 | tf_op jit(solution)/shard_map/all_to_all | solution.py:94
  634.1 0.8 broadcast_in_dim.37
  635.0 12.7 %all-to-all-start.15 = ((f32[32,16,256]{2,1,0:T(8,128)}), f32[32,16,256]{2,1,0:T(8,128)S(1)}, u32[]{:S(2)}, u32[]{:S(2)}) async-start(f32[32,16,256]{2,1,0:T(8,128)} %broadcast_in_dim.37), calls=%async_computation.15 | async-start | bytes 1048576 | tf_op jit(solution)/shard_map/all_to_all | solution.py:46
  648.2 0.9 convolution_multiply_fusion
  649.0 30.3 %all-to-all-done.15 = f32[32,16,256]{2,1,0:T(8,128)S(1)} async-done(((f32[32,16,256]{2,1,0:T(8,128)}), f32[32,16,256]{2,1,0:T(8,128)S(1)}, u32[]{:S(2)}, u32[]{:S(2)}) %all-to-all-start.15) | async-done | bytes 524320 | tf_op jit(solution)/shard_map/all_to_all | solution.py:46
  680.3 0.8 convolution_multiply_fusion.1
  (101 shorter events, 7.5 us)
Async XLA Ops:
  0.6 69.8 %copy-start = (bf16[256,2048]{1,0:T(8,128)(2,1)S(1)}, bf16[256,2048]{1,0:T(8,128)(2,1)}, u32[]{:S(2)}) copy-start(bf16[256,2048]{1,0:T(8,128)(2,1)} %param.7) | copy-start | bytes 3145732
  64.8 5.6 copy-start.1
  606.5 27.6 %all-to-all-start.16 = ((bf16[16,128,128]{2,1,0:T(8,128)(2,1)}), bf16[16,128,128]{2,1,0:T(8,128)(2,1)S(1)}, u32[]{:S(2)}, u32[]{:S(2)}) async-start(bf16[16,128,128]{2,1,0:T(8,128)(2,1)} %bitcast.39), calls=%async_computation.16 | async-start | bytes 1048576 | tf_op jit(solution)/shard_map/all_to_all | solution.py:94
  635.0 12.7 %copy-start.2 = (s32[4]{0:T(128)S(1)}, s32[4]{0:T(128)}, u32[]{:S(2)}) copy-start(s32[4]{0:T(128)} %param.10) | copy-start | bytes 52
  635.0 44.3 %all-to-all-start.15 = ((f32[32,16,256]{2,1,0:T(8,128)}), f32[32,16,256]{2,1,0:T(8,128)S(1)}, u32[]{:S(2)}, u32[]{:S(2)}) async-start(f32[32,16,256]{2,1,0:T(8,128)} %broadcast_in_dim.37), calls=%async_computation.15 | async-start | bytes 1048576 | tf_op jit(solution)/shard_map/all_to_all | solution.py:46
